TPU v7x, 32 devices: a whole 2x2x4 slice. The times are simulated.
32 devices in a mesh: dp: 8 (over z, x), rep: 4 (over y, core).
Axes of the slice: x: 2, y: 2, z: 4, core: 2. Of those that a mesh axis runs over, the one named last changes fastest.
Arguments:
- token_inputs: bfloat16 [16384, 2048], P(('dp', 'rep')), may hold values from -12 to 12
- cotangent: bfloat16 [16384, 2048], P(('dp', 'rep')), may hold values from -6 to 6
- gate_preact: bfloat16 [16384, 768], P(('dp', 'rep')), may hold values from -6 to 6
- up_preact: bfloat16 [16384, 768], P(('dp', 'rep')), may hold values from -6 to 6
- down_weight: bfloat16 [2, 768, 2048], P(None, None, 'dp'), may hold values from -0.21875 to 0.21875
- block_expert: int32 [128], P(('dp', 'rep')), may hold values from 0 to 1
- block_count: int32 [128], P(('dp', 'rep')), may hold values from 1 to 128, as said below
Outputs:
- update: bfloat16 [2, 3, 768, 2048], P(None, None, None, 'dp')
Inputs may be any that keep to these rules, and one draw needn't show every extreme that they name: `block_count`: live rows of a block, at most 128; in every draw some block is full.
All inputs are finite; a program needn't handle non-finite values.
Results may differ from a plain program's by a relative error of at most 0.02.
Values may be sent and summed in bfloat16 or wider, within the bound.
A program may use at most 128 MiB of HBM per device.

v0:
```python
import math
import jax
import jax.numpy as jnp
from jax import lax
from jax.sharding import PartitionSpec as P

D = 2048
ITERS = 2
ns_first = 3.4445
ns_second = -4.775
ns_third = 2.0315
norm_eps = 1e-07


def whole_sweeps(matrix, column_width, groups_all, sweeps, scale):
    hidden_width = matrix.shape[0]
    group = math.gcd(8, groups_all)
    current = matrix
    result = None
    for sweep in range(sweeps):

        def add_group(index, total):
            cols = lax.dynamic_slice_in_dim(
                current, index * group * column_width, group * column_width, 1
            )
            cols = cols.reshape(hidden_width, group, column_width)
            term = jnp.einsum(
                "fnd,gnd->nfg", cols, cols, preferred_element_type=jnp.float32
            ).astype(jnp.bfloat16)
            return total + jnp.sum(lax.optimization_barrier(term).astype(jnp.float32), axis=0)

        gram = lax.fori_loop(
            0, groups_all // group, add_group, jnp.zeros((hidden_width, hidden_width), jnp.float32)
        )
        gram_half = gram.astype(jnp.bfloat16)
        squared = jnp.dot(gram_half, gram_half, preferred_element_type=jnp.float32)
        poly = (ns_second * gram + ns_third * squared).astype(jnp.bfloat16)
        newer = ns_first * current.astype(jnp.float32) + jnp.dot(
            poly, current, preferred_element_type=jnp.float32
        )
        if sweep + 1 < sweeps:
            current = newer.astype(jnp.bfloat16)
        else:
            result = (scale * newer).astype(jnp.bfloat16)
    return result


def per_device(
    token_inputs, cotangent, gate_preact, up_preact, down_weight, block_expert, block_count
):
    blocks = block_count.shape[0]
    rows_here = token_inputs.shape[0]
    hidden_width = gate_preact.shape[1]
    width = token_inputs.shape[1]
    block_rows = rows_here // blocks
    experts_here = down_weight.shape[0]
    row_place = jnp.arange(rows_here, dtype=jnp.int32) % block_rows
    row_count = jnp.repeat(block_count, block_rows, total_repeat_length=rows_here)
    row_expert = jnp.repeat(block_expert, block_rows, total_repeat_length=rows_here)
    live_rows = row_place < row_count
    masked = jnp.where(live_rows[:, None], cotangent, jnp.zeros_like(cotangent))
    gate = gate_preact.astype(jnp.float32)
    upper = up_preact.astype(jnp.float32)
    sigmoid_gate = jax.nn.sigmoid(gate)
    hidden = (gate * sigmoid_gate * upper).astype(jnp.bfloat16)
    selector = (row_expert[None, :] == jnp.arange(experts_here, dtype=jnp.int32)[:, None]).astype(
        jnp.bfloat16
    )
    masked_each = masked[None, :, :] * selector[:, :, None]
    weights_all = lax.all_gather(down_weight, "dp", axis=2, tiled=True)
    back = jnp.einsum("erd,efd->rf", masked_each, weights_all, preferred_element_type=jnp.float32)
    grad_gate = (back * upper * sigmoid_gate * (1.0 + gate * (1.0 - sigmoid_gate))).astype(
        jnp.bfloat16
    )
    grad_up = (back * gate * sigmoid_gate).astype(jnp.bfloat16)
    gate_up = jnp.concatenate([grad_gate, grad_up], axis=1)
    gate_up_each = gate_up[None, :, :] * selector[:, :, None]
    hidden_each = hidden[None, :, :] * selector[:, :, None]
    input_part = jnp.einsum(
        "erf,rd->efd", gate_up_each, token_inputs, preferred_element_type=jnp.float32
    )
    output_part = jnp.einsum("erf,rd->efd", hidden_each, masked, preferred_element_type=jnp.float32)
    partial_value = jnp.concatenate(
        [input_part.reshape(experts_here, 2, hidden_width, width), output_part[:, None]], axis=1
    )
    partial_half = partial_value.astype(jnp.bfloat16)
    terms = lax.optimization_barrier(partial_half).astype(jnp.float32)
    grad = lax.psum_scatter(
        terms.astype(jnp.bfloat16), "dp", scatter_dimension=3, tiled=True
    ).astype(jnp.float32)
    grad = lax.psum(grad.astype(jnp.bfloat16), "rep").astype(jnp.float32)
    squares = lax.psum(jnp.sum(grad * grad, axis=(2, 3)), "dp")
    current = (grad / (jnp.sqrt(squares) + norm_eps)[:, :, None, None]).astype(jnp.bfloat16)
    column_width = current.shape[3]
    scale = jnp.sqrt(jnp.float32(D))
    result = None
    n_dp = lax.axis_size("dp")
    matrices = experts_here * 3
    flat = current.reshape(matrices, hidden_width, column_width)
    padding = jnp.zeros((n_dp - matrices, hidden_width, column_width), jnp.bfloat16)
    outbound = jnp.concatenate([flat, padding], axis=0)
    owned = lax.all_to_all(outbound, "dp", split_axis=0, concat_axis=2, tiled=True)
    finished = whole_sweeps(owned[0], column_width, n_dp, ITERS, scale)
    returned = lax.all_to_all(finished[None], "dp", split_axis=2, concat_axis=0, tiled=True)
    result = returned[:matrices].reshape(experts_here, 3, hidden_width, column_width)
    return result


def solution(mesh):
    placed = (
        P(("dp", "rep"), None),
        P(("dp", "rep"), None),
        P(("dp", "rep"), None),
        P(("dp", "rep"), None),
        P(None, None, "dp"),
        P(("dp", "rep")),
        P(("dp", "rep")),
    )
    return jax.shard_map(
        per_device, mesh=mesh, in_specs=placed, out_specs=P(None, None, None, "dp"), check_vma=False
    )
```

profile of v0, /device:TPU:0, one launch (start us, length us, event | category | flops | bytes accessed | tf_op | source)
XLA Modules:
  0.0 795.3 jit_solution(15564926438498596758)
XLA Ops:
  15.2 3.1 broadcast_select_fusion
  18.3 93.3 %all-gather.2.cloned.1.call-done = bf16[2,768,2048]{2,1,0:T(8,128)(2,1)} async-done(((bf16[2,768,256]{2,1,0:T(8,128)(2,1)}), bf16[2,768,2048]{2,1,0:T(8,128)(2,1)}) %all-gather.2.cloned.1.call-update) | async-done | bytes 6291472 | tf_op jit(solution)/shard_map/all_gather | solution.py:70
  111.6 7.8 fusion.15
  124.5 5.5 convert_bitcast_fusion
  130.0 6.9 convolution_convert_fusion
  136.9 10.4 %pad_maximum_fusion = bf16[2,3,768,2048]{3,2,1,0:T(8,128)(2,1)} fusion(bf16[2,1,768,2048]{3,2,1,0:T(8,128)(2,1)S(1)} %convert_bitcast_fusion, bf16[2,2,768,2048]{3,2,1,0:T(8,128)(2,1)S(1)} %bitcast.77), kind=kLoop, calls=%fused_computation | loop fusion | flops 9437184 | bytes 37748736 | tf_op jit(solution)/shard_map/concatenate | solution.py:83
  147.4 308.6 %reduce-scatter.2.cloned.1.call-done = bf16[2,3,768,256]{3,2,1,0:T(8,128)(2,1)} async-done(((bf16[2,3,768,2048]{3,2,1,0:T(8,128)(2,1)}), bf16[2,3,768,256]{3,2,1,0:T(8,128)(2,1)}) %reduce-scatter.2.cloned.1.call-update) | async-done | bytes 2359312 | tf_op jit(solution)/shard_map/reduce_scatter | solution.py:88
  456.1 57.2 %all-reduce.3.cloned.1.call-done = bf16[2,3,768,256]{3,2,1,0:T(8,128)(2,1)} async-done(((bf16[2,3,768,256]{3,2,1,0:T(8,128)(2,1)}), bf16[2,3,768,256]{3,2,1,0:T(8,128)(2,1)}) %all-reduce.3.cloned.1.call-update) | async-done | bytes 2359312 | tf_op jit(solution)/shard_map/psum | solution.py:91
  515.7 21.3 %psum.15 = f32[2,3]{1,0:T(2,128)S(1)} all-reduce(f32[2,3]{1,0:T(2,128)S(1)} %fusion), channel_id=1, replica_groups=mesh['dp'=8,'rep'=4] {'dp'}, use_global_device_ids=true, to_apply=%region_3.5 | all-reduce | flops 6 | bytes 48 | tf_op jit(solution)/shard_map/psum | solution.py:92
  538.2 70.2 %all_to_all.30 = bf16[8,768,256]{2,1,0:T(8,128)(2,1)} all-to-all(bf16[8,768,256]{2,1,0:T(8,128)(2,1)S(1)} %concatenate.18), channel_id=1, replica_groups=mesh['dp'=8,'rep'=4] {'dp'}, dimensions={0} | all-to-all | bytes 6291456 | tf_op jit(solution)/shard_map/all_to_all | solution.py:102
  608.4 5.5 convolution_convert_fusion.2
  616.6 3.2 copy.34
  619.8 3.0 copy.35
  622.8 9.3 %add_convert_fusion = bf16[768,2048]{1,0:T(8,128)(2,1)} fusion(bf16[768,2048]{1,0:T(8,128)(2,1)} %copy.35, bf16[768,2048]{0,1:T(8,128)(2,1)S(1)} %bitcast.76, f32[768,768]{1,0:T(8,128)} %convert_reduce_fusion.1), kind=kOutput, calls=%fused_computation.7 | convolution fusion | flops 3331129344 | bytes 11796480 | tf_op jit(solution)/shard_map/dot_general | solution.py:38
  632.1 5.5 convolution_convert_fusion.1
  637.6 2.7 convert_reduce_fusion
  640.4 8.7 %fusion.8 = bf16[1,768,2048]{2,1,0:T(8,128)(2,1)S(1)} fusion(bf16[768,2048]{1,0:T(8,128)(2,1)} %add_convert_fusion, f32[768,768]{1,0:T(8,128)} %convert_reduce_fusion), kind=kOutput, calls=%fused_computation.19 | convolution fusion | flops 3332702208 | bytes 8650752 | tf_op jit(solution)/shard_map/dot_general | solution.py:38
  649.1 11.2 %copy.38 = bf16[1,768,2048]{1,0,2:T(2,128)(2,1)} copy(bf16[1,768,2048]{2,1,0:T(8,128)(2,1)S(1)} %fusion.8) | data formatting | bytes 6291456 | tf_op jit(solution)/shard_map/broadcast_in_dim | solution.py:104
  660.8 33.5 %reduce.3 = bf16[2048,768]{1,0:T(8,128)(2,1)} reduce(bf16[2048,1,768]{2,1,0:T(2,128)(2,1)} %bitcast.73, bf16[]{:T(256)} %broadcast.198), dimensions={1}, to_apply=%bitcast.67.reduce_sub_computation | reduce | bytes 6291458
  694.3 4.6 reshape.141
  699.0 72.8 %all_to_all.31 = bf16[8,2,98304]{2,1,0:T(2,128)(2,1)} all-to-all(bf16[8,2,98304]{2,1,0:T(2,128)(2,1)S(1)} %reshape.141), channel_id=1, replica_groups=mesh['dp'=8,'rep'=4] {'dp'}, dimensions={0} | all-to-all | bytes 6291456 | tf_op jit(solution)/shard_map/all_to_all | solution.py:104
  771.8 7.8 reshape.142
  779.6 3.3 copy.40
  784.5 4.3 copy.39
  (29 shorter events, 22.1 us)
Async XLA Ops:
  6.5 123.4 %copy-start = (bf16[512,2048]{1,0:T(8,128)(2,1)S(1)}, bf16[512,2048]{1,0:T(8,128)(2,1)}, u32[]{:S(2)}) copy-start(bf16[512,2048]{1,0:T(8,128)(2,1)} %param.13) | copy-start | bytes 6291460
  6.5 105.1 %all-gather.2.cloned.1.call-start = ((), (), s32[]{:S(2)}) async-start(), calls=%async_computation.3 | async-start | bytes 7077888 | tf_op jit(solution)/shard_map/all_gather | solution.py:70
  7.3 448.8 %reduce-scatter.2.cloned.1.call-start = ((), (), s32[]{:S(2)}) async-start(), calls=%async_computation.4 | async-start | bytes 21233664 | tf_op jit(solution)/shard_map/reduce_scatter | solution.py:88
  124.5 5.5 copy-start.3
  147.4 365.9 %all-reduce.3.cloned.1.call-start = ((), (), s32[]{:S(2)}) async-start(), calls=%async_computation.5 | async-start | bytes 4718592 | tf_op jit(solution)/shard_map/psum | solution.py:91
  513.2 23.8 %copy-start.2 = (bf16[2,3,768,256]{3,2,1,0:T(8,128)(2,1)S(1)}, bf16[2,3,768,256]{3,2,1,0:T(8,128)(2,1)}, u32[]{:S(2)}) copy-start(bf16[2,3,768,256]{3,2,1,0:T(8,128)(2,1)} %all-reduce.3.cloned.1.call-done) | copy-start | bytes 7077892
  782.9 5.9 copy-start.1
Sparse Core Ops, SparseCore 0:
  9.4 102.1 all-gather.1
  147.5 308.5 reduce-scatter.1
  458.4 54.7 all-reduce.2
where the time goes:
time: 796 us; the launch traced here: 795 us
  waiting for transfers between devices  460 us (58%)
  blocking collectives  164 us (21%)
  other arithmetic  62.2 us (8%)
  matrix products  49.3 us (6%)
  local copies, waits for them, and re-layouts  46.3 us (6%)
  between operations  13.2 us (2%)
    reduce_scatter x1, waiting for transfers between devices, per_device(): lax.psum_scatter(terms.astype(jnp.bfloat16), 'dp', scatter_dimension=3, t...  309 us
    all_gather x1, waiting for transfers between devices, per_device(): weights_all = lax.all_gather(down_weight, 'dp', axis=2, tiled=True)  93.3 us
    all_to_all x1, blocking collectives, per_device(): lax.all_to_all(finished[None], 'dp', split_axis=2, concat_axis=0, tiled=T...  72.8 us
    all_to_all x1, blocking collectives, per_device(): lax.all_to_all(outbound, 'dp', split_axis=0, concat_axis=2, tiled=True)  70.2 us
    psum x1, waiting for transfers between devices, per_device(): grad = lax.psum(grad.astype(jnp.bfloat16), 'rep').astype(jnp.float32)  57.2 us
    unnamed x1, other arithmetic  33.5 us
    psum x1, blocking collectives, per_device(): squares = lax.psum(jnp.sum(grad * grad, axis=(2, 3)), 'dp')  21.3 us
    dot_general x2, matrix products, whole_sweeps(): jnp.dot(poly, current, preferred_element_type=jnp.float32)  18 us
  transfers between devices with their start and end apart: 3, of which 3 were waited for; matrix products, arithmetic and copies ran while one was open for 1% of the time, Pallas kernels for 0%

commit v1 on v0

--- a/solution.py
+++ b/solution.py
@@ -10,6 +10,21 @@
 ns_second = -4.775
 ns_third = 2.0315
 norm_eps = 1e-07
+
+
+def divide_row_in(s0, row_axis, d_out):
+    shares = lax.axis_size(row_axis)
+    block_list = tuple(((at, (at + 1) % shares) for at in range(shares)))
+
+    def series_map(kept_arr):
+        if len(kept_arr) == shares:
+            return kept_arr
+        plain = series_map([lax.ppermute(kept_arr[0], row_axis, block_list), *kept_arr])
+        return plain
+
+    before = jnp.concatenate(series_map([s0]), axis=d_out)
+    newest = jnp.roll(before, shift=(lax.axis_index(row_axis) + 1) * s0.shape[d_out], axis=d_out)
+    return newest
 
 
 def whole_sweeps(matrix, column_width, groups_all, sweeps, scale):
@@ -67,7 +82,7 @@
         jnp.bfloat16
     )
     masked_each = masked[None, :, :] * selector[:, :, None]
-    weights_all = lax.all_gather(down_weight, "dp", axis=2, tiled=True)
+    weights_all = divide_row_in(down_weight, "dp", 2)
     back = jnp.einsum("erd,efd->rf", masked_each, weights_all, preferred_element_type=jnp.float32)
     grad_gate = (back * upper * sigmoid_gate * (1.0 + gate * (1.0 - sigmoid_gate))).astype(
         jnp.bfloat16

time: 796 us -> 838 us (1.053)
  waiting for transfers between devices: 460 us -> 491 us
  local copies, waits for them, and re-layouts: 46.3 us -> 57.7 us
    ppermute x0 -> x7, waiting for transfers between devices: none -> 127 us  [series_map(): lax.ppermute(kept_arr[0], row_axis, block_list)]
    all_gather x1 -> x0, waiting for transfers between devices: 93.3 us -> none  [per_device(): weights_all = lax.all_gather(down_weight, 'dp', axis=2, tiled=True)]
    unnamed x12 -> x51, local copies, waits for them, and re-layouts: 16.2 us -> 27.5 us
  transfers between devices with their start and end apart: 3 -> 9, of which waited for: 3 -> 9; matrix products, arithmetic and copies ran while one was open for 1% -> 1% of each run, Pallas kernels for 0% -> 0%
where the time goes in v1:
time: 838 us; the launch traced here: 837 us
  waiting for transfers between devices  491 us (59%)
  blocking collectives  164 us (20%)
  other arithmetic  61.1 us (7%)
  local copies, waits for them, and re-layouts  57.7 us (7%)
  matrix products  45.5 us (5%)
  between operations  13.8 us (2%)
    reduce_scatter x1, waiting for transfers between devices, per_device(): lax.psum_scatter(terms.astype(jnp.bfloat16), 'dp', scatter_dimension=3, t...  307 us
    ppermute x7, waiting for transfers between devices, series_map(): lax.ppermute(kept_arr[0], row_axis, block_list)  127 us
    all_to_all x1, blocking collectives, per_device(): lax.all_to_all(finished[None], 'dp', split_axis=2, concat_axis=0, tiled=T...  72.8 us
    all_to_all x1, blocking collectives, per_device(): lax.all_to_all(outbound, 'dp', split_axis=0, concat_axis=2, tiled=True)  70.2 us
    psum x1, waiting for transfers between devices, per_device(): grad = lax.psum(grad.astype(jnp.bfloat16), 'rep').astype(jnp.float32)  57.1 us
    unnamed x1, other arithmetic  33.6 us
    unnamed x51, local copies, waits for them, and re-layouts  27.5 us
    psum x1, blocking collectives, per_device(): squares = lax.psum(jnp.sum(grad * grad, axis=(2, 3)), 'dp')  21.3 us
  transfers between devices with their start and end apart: 9, of which 9 were waited for; matrix products, arithmetic and copies ran while one was open for 1% of the time, Pallas kernels for 0%

profile of v1, /device:TPU:0, one launch (start us, length us, event | category | flops | bytes accessed | tf_op | source)
XLA Modules:
  0.0 836.8 jit_solution(1983767858085236049)
XLA Ops:
  9.5 20.8 %collective-permute-done = bf16[2,768,256]{2,1,0:T(8,128)(2,1)S(1)} collective-permute-done((bf16[2,768,256]{2,1,0:T(8,128)(2,1)}, bf16[2,768,256]{2,1,0:T(8,128)(2,1)S(1)}, u32[]{:S(2)}, u32[]{:S(2)}) %collective-permute-start) | collective-permute-done | bytes 786464 | tf_op jit(solution)/shard_map/ppermute | solution.py:22
  30.3 21.4 %collective-permute-done.1 = bf16[2,768,256]{2,1,0:T(8,128)(2,1)S(1)} collective-permute-done((bf16[2,768,256]{2,1,0:T(8,128)(2,1)S(1)}, bf16[2,768,256]{2,1,0:T(8,128)(2,1)S(1)}, u32[]{:S(2)}, u32[]{:S(2)}) %collective-permute-start.1) | collective-permute-done | bytes 786464 | tf_op jit(solution)/shard_map/ppermute | solution.py:22
  52.6 20.5 %collective-permute-done.2 = bf16[2,768,256]{2,1,0:T(8,128)(2,1)S(1)} collective-permute-done((bf16[2,768,256]{2,1,0:T(8,128)(2,1)S(1)}, bf16[2,768,256]{2,1,0:T(8,128)(2,1)S(1)}, u32[]{:S(2)}, u32[]{:S(2)}) %collective-permute-start.2) | collective-permute-done | bytes 786464 | tf_op jit(solution)/shard_map/ppermute | solution.py:22
  74.0 19.7 %collective-permute-done.3 = bf16[2,768,256]{2,1,0:T(8,128)(2,1)S(1)} collective-permute-done((bf16[2,768,256]{2,1,0:T(8,128)(2,1)S(1)}, bf16[2,768,256]{2,1,0:T(8,128)(2,1)S(1)}, u32[]{:S(2)}, u32[]{:S(2)}) %collective-permute-start.3) | collective-permute-done | bytes 786464 | tf_op jit(solution)/shard_map/ppermute | solution.py:22
  94.6 18.8 %collective-permute-done.4 = bf16[2,768,256]{2,1,0:T(8,128)(2,1)S(1)} collective-permute-done((bf16[2,768,256]{2,1,0:T(8,128)(2,1)S(1)}, bf16[2,768,256]{2,1,0:T(8,128)(2,1)S(1)}, u32[]{:S(2)}, u32[]{:S(2)}) %collective-permute-start.4) | collective-permute-done | bytes 786464 | tf_op jit(solution)/shard_map/ppermute | solution.py:22
  119.9 12.5 %collective-permute-done.5 = bf16[2,768,256]{2,1,0:T(8,128)(2,1)} collective-permute-done((bf16[2,768,256]{2,1,0:T(8,128)(2,1)S(1)}, bf16[2,768,256]{2,1,0:T(8,128)(2,1)}, u32[]{:S(2)}, u32[]{:S(2)}) %collective-permute-start.5) | collective-permute-done | bytes 786464 | tf_op jit(solution)/shard_map/ppermute | solution.py:22
  136.9 13.0 %collective-permute-done.6 = bf16[2,768,256]{2,1,0:T(8,128)(2,1)} collective-permute-done((bf16[2,768,256]{2,1,0:T(8,128)(2,1)}, bf16[2,768,256]{2,1,0:T(8,128)(2,1)}, u32[]{:S(2)}, u32[]{:S(2)}) %collective-permute-start.6) | collective-permute-done | bytes 786464 | tf_op jit(solution)/shard_map/ppermute | solution.py:22
  167.1 5.5 convert_bitcast_fusion
  172.6 6.9 convolution_convert_fusion
  179.5 10.4 %pad_maximum_fusion = bf16[2,3,768,2048]{3,2,1,0:T(8,128)(2,1)} fusion(bf16[2,1,768,2048]{3,2,1,0:T(8,128)(2,1)S(1)} %convert_bitcast_fusion, bf16[2,2,768,2048]{3,2,1,0:T(8,128)(2,1)S(1)} %bitcast.76), kind=kLoop, calls=%fused_computation | loop fusion | flops 9437184 | bytes 37748736 | tf_op jit(solution)/shard_map/concatenate | solution.py:98
  190.2 307.1 %reduce-scatter.2.cloned.1.call-done = bf16[2,3,768,256]{3,2,1,0:T(8,128)(2,1)} async-done(((bf16[2,3,768,2048]{3,2,1,0:T(8,128)(2,1)}), bf16[2,3,768,256]{3,2,1,0:T(8,128)(2,1)}) %reduce-scatter.2.cloned.1.call-update) | async-done | bytes 2359312 | tf_op jit(solution)/shard_map/reduce_scatter | solution.py:103
  497.4 57.1 %all-reduce.3.cloned.1.call-done = bf16[2,3,768,256]{3,2,1,0:T(8,128)(2,1)} async-done(((bf16[2,3,768,256]{3,2,1,0:T(8,128)(2,1)}), bf16[2,3,768,256]{3,2,1,0:T(8,128)(2,1)}) %all-reduce.3.cloned.1.call-update) | async-done | bytes 2359312 | tf_op jit(solution)/shard_map/psum | solution.py:106
  557.0 21.3 %psum.15 = f32[2,3]{1,0:T(2,128)S(1)} all-reduce(f32[2,3]{1,0:T(2,128)S(1)} %fusion.2), channel_id=1, replica_groups=mesh['dp'=8,'rep'=4] {'dp'}, use_global_device_ids=true, to_apply=%region_3.5 | all-reduce | flops 6 | bytes 48 | tf_op jit(solution)/shard_map/psum | solution.py:107
  579.5 70.2 %all_to_all.30 = bf16[8,768,256]{2,1,0:T(8,128)(2,1)} all-to-all(bf16[8,768,256]{2,1,0:T(8,128)(2,1)S(1)} %concatenate.25), channel_id=1, replica_groups=mesh['dp'=8,'rep'=4] {'dp'}, dimensions={0} | all-to-all | bytes 6291456 | tf_op jit(solution)/shard_map/all_to_all | solution.py:117
  649.7 5.5 convolution_convert_fusion.2
  664.1 9.3 %add_convert_fusion = bf16[768,2048]{1,0:T(8,128)(2,1)} fusion(bf16[768,2048]{1,0:T(8,128)(2,1)} %copy.35, bf16[768,2048]{0,1:T(8,128)(2,1)S(1)} %bitcast.75, f32[768,768]{1,0:T(8,128)} %convert_reduce_fusion.1), kind=kOutput, calls=%fused_computation.7 | convolution fusion | flops 3331129344 | bytes 11796480 | tf_op jit(solution)/shard_map/dot_general | solution.py:53
  673.4 5.5 convolution_convert_fusion.1
  681.6 8.6 %fusion.9 = bf16[1,768,2048]{2,1,0:T(8,128)(2,1)S(1)} fusion(bf16[768,2048]{1,0:T(8,128)(2,1)} %add_convert_fusion, f32[768,768]{1,0:T(8,128)} %convert_reduce_fusion), kind=kOutput, calls=%fused_computation.20 | convolution fusion | flops 3332702208 | bytes 8650752 | tf_op jit(solution)/shard_map/dot_general | solution.py:53
  690.2 11.2 %copy.38 = bf16[1,768,2048]{1,0,2:T(2,128)(2,1)} copy(bf16[1,768,2048]{2,1,0:T(8,128)(2,1)S(1)} %fusion.9) | data formatting | bytes 6291456 | tf_op jit(solution)/shard_map/broadcast_in_dim | solution.py:119
  702.0 33.6 %reduce.3 = bf16[2048,768]{1,0:T(8,128)(2,1)} reduce(bf16[2048,1,768]{2,1,0:T(2,128)(2,1)} %bitcast.72, bf16[]{:T(256)} %broadcast.199), dimensions={1}, to_apply=%bitcast.67.reduce_sub_computation | reduce | bytes 6291458
  735.5 4.6 reshape.141
  740.2 72.8 %all_to_all.31 = bf16[8,2,98304]{2,1,0:T(2,128)(2,1)} all-to-all(bf16[8,2,98304]{2,1,0:T(2,128)(2,1)S(1)} %reshape.141), channel_id=1, replica_groups=mesh['dp'=8,'rep'=4] {'dp'}, dimensions={0} | all-to-all | bytes 6291456 | tf_op jit(solution)/shard_map/all_to_all | solution.py:119
  813.0 7.8 reshape.142
  825.6 4.3 copy.39
  (80 shorter events, 54.4 us)
Async XLA Ops:
  6.5 166.0 %copy-start = (bf16[512,2048]{1,0:T(8,128)(2,1)S(1)}, bf16[512,2048]{1,0:T(8,128)(2,1)}, u32[]{:S(2)}) copy-start(bf16[512,2048]{1,0:T(8,128)(2,1)} %param.13) | copy-start | bytes 6291460
  6.5 490.8 %reduce-scatter.2.cloned.1.call-start = ((), (), s32[]{:S(2)}) async-start(), calls=%async_computation.3 | async-start | bytes 21233664 | tf_op jit(solution)/shard_map/reduce_scatter | solution.py:103
  6.5 23.8 %collective-permute-start = (bf16[2,768,256]{2,1,0:T(8,128)(2,1)}, bf16[2,768,256]{2,1,0:T(8,128)(2,1)S(1)}, u32[]{:S(2)}, u32[]{:S(2)}) collective-permute-start(bf16[2,768,256]{2,1,0:T(8,128)(2,1)} %param.17), channel_id=1, source_target_pairs={{0,4},{4,8},{8,12},{12,16},{16,20},{20,24},{24,28},{28,0},{1,5},{5... | collective-permute-start | bytes 2359304 | tf_op jit(solution)/shard_map/ppermute | solution.py:22
  30.3 21.4 %collective-permute-start.1 = (bf16[2,768,256]{2,1,0:T(8,128)(2,1)S(1)}, bf16[2,768,256]{2,1,0:T(8,128)(2,1)S(1)}, u32[]{:S(2)}, u32[]{:S(2)}) collective-permute-start(bf16[2,768,256]{2,1,0:T(8,128)(2,1)S(1)} %collective-permute-done), channel_id=1, source_target_pairs={{0,4},{4,8},{8,12},{12,16},{16,20},{20,24},{24,28},{28,0},{1,5},{5... | collective-permute-start | bytes 2359304 | tf_op jit(solution)/shard_map/ppermute | solution.py:22
  51.7 0.9 copy-start.4
  52.6 20.5 %collective-permute-start.2 = (bf16[2,768,256]{2,1,0:T(8,128)(2,1)S(1)}, bf16[2,768,256]{2,1,0:T(8,128)(2,1)S(1)}, u32[]{:S(2)}, u32[]{:S(2)}) collective-permute-start(bf16[2,768,256]{2,1,0:T(8,128)(2,1)S(1)} %collective-permute-done.1), channel_id=1, source_target_pairs={{0,4},{4,8},{8,12},{12,16},{16,20},{20,24},{24,28},{28,0},{1,5},{5... | collective-permute-start | bytes 2359304 | tf_op jit(solution)/shard_map/ppermute | solution.py:22
  74.0 19.7 %collective-permute-start.3 = (bf16[2,768,256]{2,1,0:T(8,128)(2,1)S(1)}, bf16[2,768,256]{2,1,0:T(8,128)(2,1)S(1)}, u32[]{:S(2)}, u32[]{:S(2)}) collective-permute-start(bf16[2,768,256]{2,1,0:T(8,128)(2,1)S(1)} %collective-permute-done.2), channel_id=1, source_target_pairs={{0,4},{4,8},{8,12},{12,16},{16,20},{20,24},{24,28},{28,0},{1,5},{5... | collective-permute-start | bytes 2359304 | tf_op jit(solution)/shard_map/ppermute | solution.py:22
  93.7 0.9 copy-start.8
  94.6 18.8 %collective-permute-start.4 = (bf16[2,768,256]{2,1,0:T(8,128)(2,1)S(1)}, bf16[2,768,256]{2,1,0:T(8,128)(2,1)S(1)}, u32[]{:S(2)}, u32[]{:S(2)}) collective-permute-start(bf16[2,768,256]{2,1,0:T(8,128)(2,1)S(1)} %collective-permute-done.3), channel_id=1, source_target_pairs={{0,4},{4,8},{8,12},{12,16},{16,20},{20,24},{24,28},{28,0},{1,5},{5... | collective-permute-start | bytes 2359304 | tf_op jit(solution)/shard_map/ppermute | solution.py:22
  113.4 0.9 copy-start.10
  114.3 18.1 %collective-permute-start.5 = (bf16[2,768,256]{2,1,0:T(8,128)(2,1)S(1)}, bf16[2,768,256]{2,1,0:T(8,128)(2,1)}, u32[]{:S(2)}, u32[]{:S(2)}) collective-permute-start(bf16[2,768,256]{2,1,0:T(8,128)(2,1)S(1)} %collective-permute-done.4), channel_id=1, source_target_pairs={{0,4},{4,8},{8,12},{12,16},{16,20},{20,24},{24,28},{28,0},{1,5},{5... | collective-permute-start | bytes 2359304 | tf_op jit(solution)/shard_map/ppermute | solution.py:22
  132.4 17.4 %collective-permute-start.6 = (bf16[2,768,256]{2,1,0:T(8,128)(2,1)}, bf16[2,768,256]{2,1,0:T(8,128)(2,1)}, u32[]{:S(2)}, u32[]{:S(2)}) collective-permute-start(bf16[2,768,256]{2,1,0:T(8,128)(2,1)} %collective-permute-done.5), channel_id=1, source_target_pairs={{0,4},{4,8},{8,12},{12,16},{16,20},{20,24},{24,28},{28,0},{1,5},{5... | collective-permute-start | bytes 2359304 | tf_op jit(solution)/shard_map/ppermute | solution.py:22
  135.0 17.4 %copy-start.11 = (bf16[2,768,256]{2,1,0:T(8,128)(2,1)S(1)}, bf16[2,768,256]{2,1,0:T(8,128)(2,1)}, u32[]{:S(2)}) copy-start(bf16[2,768,256]{2,1,0:T(8,128)(2,1)} %copy-done.10) | copy-start | bytes 2359300
  136.8 20.1 %copy-start.12 = (bf16[512,2048]{1,0:T(8,128)(2,1)}, bf16[512,2048]{1,0:T(8,128)(2,1)S(1)}, u32[]{:S(2)}) copy-start(bf16[512,2048]{1,0:T(8,128)(2,1)S(1)} %broadcast_select_fusion) | copy-start | bytes 6291460
  136.9 15.7 %copy-start.9 = (bf16[2,768,256]{2,1,0:T(8,128)(2,1)S(1)}, bf16[2,768,256]{2,1,0:T(8,128)(2,1)}, u32[]{:S(2)}) copy-start(bf16[2,768,256]{2,1,0:T(8,128)(2,1)} %copy-done.8) | copy-start | bytes 2359300
  136.9 15.8 %copy-start.7 = (bf16[2,768,256]{2,1,0:T(8,128)(2,1)S(1)}, bf16[2,768,256]{2,1,0:T(8,128)(2,1)}, u32[]{:S(2)}) copy-start(bf16[2,768,256]{2,1,0:T(8,128)(2,1)} %copy-done.6) | copy-start | bytes 2359300
  151.1 1.7 copy-start.5
  152.5 1.1 copy-start.3
  156.5 1.1 copy-start.14
  156.5 1.4 copy-start.15
  167.1 5.5 copy-start.13
  190.0 364.5 %all-reduce.3.cloned.1.call-start = ((), (), s32[]{:S(2)}) async-start(), calls=%async_computation.4 | async-start | bytes 4718592 | tf_op jit(solution)/shard_map/psum | solution.py:106
  554.5 23.8 %copy-start.2 = (bf16[2,3,768,256]{3,2,1,0:T(8,128)(2,1)S(1)}, bf16[2,3,768,256]{3,2,1,0:T(8,128)(2,1)}, u32[]{:S(2)}) copy-start(bf16[2,3,768,256]{3,2,1,0:T(8,128)(2,1)} %all-reduce.3.cloned.1.call-done) | copy-start | bytes 7077892
  824.1 5.8 copy-start.1
  (1 other events, 0.9 us)
Sparse Core Ops, SparseCore 0:
  190.1 307.1 reduce-scatter.1
  499.7 54.7 all-reduce.2
